TPU v7x, 32 devices: a whole 2x2x4 slice. The times are simulated.
32 devices in a mesh: lat: 4 (over y, x), lon: 8 (over z, core).
Axes of the slice: x: 2, y: 2, z: 4, core: 2. Of those that a mesh axis runs over, the one named last changes fastest.
Arguments:
- right_side: float32 [512, 1024], P('lat', 'lon'), may hold values from -8 to 8
- surface_term: float32 [512, 1024], P('lat', 'lon'), may hold values from 0.0002 to 0.002
- east_coupling: float32 [512, 1024], P('lat', 'lon'), may hold values from 0.3 to 3
- north_coupling: float32 [512, 1024], P('lat', 'lon'), may hold values from 0.3 to 3
- neast_coupling: float32 [512, 1024], P('lat', 'lon'), may hold values from 0.1 to 0.5
- nwest_coupling: float32 [512, 1024], P('lat', 'lon'), may hold values from 0.1 to 0.5
- land_sea: int32 [512, 1024], P('lat', 'lon'), may hold values from 0 to 1, as said below
- fold_map: int32 [1024], P('lon'), may hold values from 0 to 1023, as said below
Outputs:
- solution: float32 [512, 1024], P('lat', 'lon')
- residual: float32 [512, 1024], P('lat', 'lon')
Inputs may be any that keep to these rules, and one draw needn't show every extreme that they name: fold_map[j] = (c - j) mod 1024 for one odd c: an involution of the columns with no fixed point. land_sea is 0 or 1; land lies in bands of 8 columns, each over one range of rows.
All inputs are finite; a program needn't handle non-finite values.
Results may differ from a plain program's by a relative error of at most 0.0015.
Values sent between devices are 32-bit elements.
A program may use at most 64 MiB of HBM per device.

v0:
```python
import functools

import jax
import jax.numpy as jnp
from jax import lax
from jax.experimental import pallas as pl
from jax.experimental.pallas import tpu as pltpu
from jax.sharding import PartitionSpec as P

ITERS = 8
SUB = 8
FIELDS = 6
MESH = pl.DeviceIdType.MESH


def iota(shape, dim):
    return lax.broadcasted_iota(jnp.int32, shape, dim)


def east(x):
    return pltpu.roll(x, x.shape[-1] - 1, x.ndim - 1)


def west(x):
    return pltpu.roll(x, 1, x.ndim - 1)


def from_above(x):
    return pltpu.roll(x, SUB - 1, 0)


def from_below(x):
    return pltpu.roll(x, 1, 0)


def alternate(size):
    ring = []
    for i in range(1, size // 2 + 1):
        ring += [size - i, i]
    return list(dict.fromkeys([*ring, 0]))


def kernel(
    lat_count,
    lon_count,
    right_ref,
    surface_ref,
    east_ref,
    north_ref,
    neast_ref,
    nwest_ref,
    land_ref,
    map_ref,
    sol_out,
    res_out,
    w_e,
    w_w,
    w_n,
    w_s,
    w_ne,
    w_sw,
    w_nw,
    w_se,
    diag,
    f_a,
    f_g,
    resp0,
    resp1,
    top_resp,
    c_mid,
    c_east,
    c_west,
    y_ref,
    w_ref,
    res_ref,
    r_mid,
    y_mid,
    z_mid,
    sol_ref,
    s_mid,
    z_pair,
    k_pair,
    fields,
    given,
    land_buf,
    map_buf,
    big_msg,
    small_msg,
    big_recv,
    small_recv,
    stat_msg,
    stat_recv,
    whole,
    msg,
    recv,
    back_msg,
    back_recv,
    in_sem,
    big_send,
    big_arrive,
    small_send,
    small_arrive,
    stat_send,
    stat_arrive,
    send_sem,
    recv_sem,
    back_send,
    back_arrive,
):
    pairs = lon_count // 2
    n_own = lat_count * pairs
    lat = lax.axis_index("lat")
    lon = lax.axis_index("lon")
    pair = lon // 2
    core = lax.rem(lon, 2)
    me = lat * pairs + pair
    depth, _, width = sol_ref.shape
    rows = depth * SUB // lat_count
    subs = SUB // lat_count
    halo = ITERS
    own = 2 * width // lat_count
    big = own + halo
    rest = width - big
    left = big - rest
    band = big_msg.shape[1]
    thin = small_msg.shape[1]
    seg = band // subs
    half = depth // 2
    top = depth - 1
    odd = lax.rem(lat, 2)
    is_owner = core == 1

    lats = [lax.rem(lat + d, lat_count) for d in range(lat_count)]
    owners = [2 * lax.rem(pair + d, pairs) + 1 for d in range(pairs)]
    few = n_own <= 64
    peers = [(p, q) for q in alternate(pairs) for p in alternate(lat_count) if p or q]

    def to_owners(act):
        if few:
            for p, q in peers:
                act((lats[p], owners[q]))
            return

        def one(step, carry):
            peer = lax.rem(me + step, n_own)
            act((peer // pairs, 2 * lax.rem(peer, pairs) + 1))
            return carry

        lax.fori_loop(1, n_own, one, 0)

    left_place = (2 * core, 2 * pair + 1)
    right_place = (2 * core + 1, 2 * pair + 1)
    next_place = (lax.rem(2 * core + 2, lat_count), 2 * lax.rem(pair + core, pairs) + 1)
    back_pair = lax.rem(pair + core + pairs - 1, pairs)
    prev_place = (lax.rem(2 * core + 3, lat_count), 2 * back_pair + 1)

    barrier = pltpu.get_barrier_semaphore()

    def greet(place):
        pl.semaphore_signal(barrier, inc=1, device_id=place, device_id_type=MESH)

    @pl.when(is_owner)
    def _():
        to_owners(greet)
        last_lat = jnp.where(lat == lat_count - 1, 1, 0)
        plain = 2 * lax.rem(pair + last_lat, pairs)
        for a in range(lat_count):
            greet((a, plain))

    @pl.when(core == 0)
    def _():
        for place in (left_place, right_place, next_place, prev_place):
            greet(place)

    sources = (right_ref, surface_ref, east_ref, north_ref, neast_ref, nwest_ref)
    loads = [
        pltpu.make_async_copy(ref, given.at[i], in_sem.at[i]) for i, ref in enumerate(sources)
    ]
    loads.append(pltpu.make_async_copy(land_ref, land_buf, in_sem.at[FIELDS]))
    map_load = pltpu.make_async_copy(map_ref, map_buf, in_sem.at[FIELDS + 1])
    for copy in loads:
        copy.start()
    map_load.start()
    for copy in loads:
        copy.wait()
    map_load.wait()

    wide = iota((SUB, width), 1)
    zero = jnp.zeros((SUB, width), jnp.float32)
    for v in range(rows // SUB):
        sl = slice(v * SUB, (v + 1) * SUB)
        given[1, sl] = given[1, sl] * land_buf[sl].astype(jnp.float32)
    for s in range(subs):
        for v in range(depth // SUB):
            sl = slice(s * depth + v * SUB, s * depth + (v + 1) * SUB)
            for c in range(FIELDS // 2):
                first, second = given[2 * c, sl], given[2 * c + 1, sl]
                at = s * seg + c * depth + v * SUB
                to = slice(at, at + SUB)
                big_msg[0, to] = jnp.where(wide < big, first, pltpu.roll(second, rest, 1))
                big_msg[1, to] = jnp.where(wide >= rest, first, pltpu.roll(second, big, 1))
        for v in range(half // SUB):
            acc_l, acc_r, acc_n, acc_p = zero, zero, zero, zero
            for i in range(FIELDS):
                for e in range(2):
                    rows_at = pl.ds(s * depth + 2 * v * SUB + e, SUB, stride=2)
                    piece = given[i, rows_at, :]
                    slot = i + FIELDS * e
                    hit = wide // halo == slot
                    lane = halo * slot
                    acc_n = jnp.where(hit, pltpu.roll(piece, (lane + halo) % width, 1), acc_n)
                    moved = pltpu.roll(piece, lane, 1) if lane else piece
                    acc_p = jnp.where(hit, moved, acc_p)
                    if i % 2 == 1:
                        slot = i // 2 + FIELDS // 2 * e
                        hit = wide // left == slot
                        lane = left * slot
                        moved = pltpu.roll(piece, lane, 1) if lane else piece
                        acc_l = jnp.where(hit, moved, acc_l)
                        moved = pltpu.roll(piece, (lane + left) % width, 1)
                        acc_r = jnp.where(hit, moved, acc_r)
            at = s * seg + FIELDS // 2 * depth + v * SUB
            big_msg[0, at : at + SUB] = acc_l
            big_msg[1, at : at + SUB] = acc_r
            at = s * half + v * SUB
            small_msg[0, at : at + SUB] = acc_n
            small_msg[1, at : at + SUB] = acc_p

    here_big = pl.ds(pl.multiple_of(lat * band, SUB), band)
    here_thin = pl.ds(pl.multiple_of(lat * thin, SUB), thin)

    def big_copy(side, place):
        return pltpu.make_async_remote_copy(
            src_ref=big_msg.at[side],
            dst_ref=big_recv.at[here_big],
            send_sem=big_send.at[side],
            recv_sem=big_arrive.at[lat],
            device_id=place,
            device_id_type=MESH,
        )

    def thin_copy(side, place):
        return pltpu.make_async_remote_copy(
            src_ref=small_msg.at[side],
            dst_ref=small_recv.at[here_thin],
            send_sem=small_send.at[side],
            recv_sem=small_arrive.at[lat],
            device_id=place,
            device_id_type=MESH,
        )

    @pl.when(is_owner)
    def _():
        pl.semaphore_wait(barrier, n_own - 1 + lat_count)

    @pl.when(core == 0)
    def _():
        pl.semaphore_wait(barrier, lat_count)

    outgoing = [
        (big_copy(0, left_place), jnp.logical_and(is_owner, lat == 2)),
        (big_copy(1, right_place), jnp.logical_and(is_owner, lat == 3)),
        (thin_copy(0, next_place), None),
        (thin_copy(1, prev_place), jnp.logical_and(is_owner, lat == 1)),
    ]
    for copy, stays in outgoing:
        if stays is None:
            copy.start()
        else:
            pl.when(jnp.logical_not(stays))(copy.start)

    @pl.when(outgoing[0][1])
    def _():
        big_recv[here_big] = big_msg[0]

    @pl.when(outgoing[1][1])
    def _():
        big_recv[here_big] = big_msg[1]

    @pl.when(outgoing[3][1])
    def _():
        small_recv[here_thin] = small_msg[1]

    def back_copy(a):
        return pltpu.make_async_remote_copy(
            src_ref=back_msg.at[a * rows : (a + 1) * rows],
            dst_ref=back_recv.at[odd],
            send_sem=back_send.at[a],
            recv_sem=back_arrive.at[odd],
            device_id=(a, 2 * pair + lat // 2),
            device_id_type=MESH,
        )

    def solve_columns():
        for a in range(lat_count):

            @pl.when(jnp.logical_or(lat != a, lat < 2))
            def _(a=a):
                pltpu.make_async_remote_copy(
                    src_ref=big_msg.at[0],
                    dst_ref=big_recv.at[a * band : (a + 1) * band],
                    send_sem=big_send.at[0],
                    recv_sem=big_arrive.at[a],
                    device_id=left_place,
                    device_id_type=MESH,
                ).wait_recv()

            @pl.when(jnp.logical_or(lat != a, lat != 1))
            def _(a=a):
                pltpu.make_async_remote_copy(
                    src_ref=small_msg.at[0],
                    dst_ref=small_recv.at[a * thin : (a + 1) * thin],
                    send_sem=small_send.at[0],
                    recv_sem=small_arrive.at[a],
                    device_id=next_place,
                    device_id_type=MESH,
                ).wait_recv()

        def between(low, size):
            return (wide >= low) & (wide < low + size)

        native = between(odd * rest, big)
        side_low = (1 - odd) * (width - halo)
        inside = native | between(side_low, halo)
        main = between(left + odd * (rest - left), rest)
        edge_low = odd * (width - left)
        edge = between(edge_low, left)

        def turned(x, shift):
            return pltpu.roll(x, lax.rem(shift + 2 * width, width), 1)

        for k in range(depth):
            e = k % 2
            strip = small_recv[pl.ds(k // 2, SUB, stride=half), :]
            spill = big_recv[pl.ds(FIELDS // 2 * depth + k // 2, SUB, stride=seg), :]
            for c in range(FIELDS // 2):
                packed = big_recv[pl.ds(c * depth + k, SUB, stride=seg), :]
                out = []
                for i in (2 * c, 2 * c + 1):
                    strip_at = turned(strip, side_low - halo * (i + FIELDS * e))
                    out.append(jnp.where(inside, strip_at, 0.0))
                fields[2 * c, k] = jnp.where(native, packed, out[0])
                spill_at = turned(spill, edge_low - left * (c + FIELDS // 2 * e))
                value = jnp.where(edge, spill_at, out[1])
                fields[2 * c + 1, k] = jnp.where(main, turned(packed, big - odd * left), value)

        def field(index, k):
            if index == FIELDS:
                return jnp.where(fields[1, k] > 0.0, 1.0, 0.0)
            return fields[index, k]

        is_top = iota((SUB, width), 0) == SUB - 1

        def closed(index, k):
            value = field(index, k)
            return jnp.where(is_top, 0.0, value) if k == top else value

        def above(index, k):
            return field(index, k + 1) if k < top else from_above(field(index, 0))

        n_prev, ne_prev, nw_prev = (from_below(closed(i, top)) for i in (3, 4, 5))
        for k in range(depth):
            ocean = field(FIELDS, k)
            ocean_north = above(FIELDS, k)
            e_now, n_now, ne_now, nw_now = field(2, k), closed(3, k), closed(4, k), closed(5, k)
            we = e_now * ocean * east(ocean)
            wn = n_now * ocean * ocean_north
            wne = ne_now * ocean * east(ocean_north)
            wnw = nw_now * ocean * west(ocean_north)
            w_e[k] = we
            w_w[k] = west(we)
            w_n[k] = wn
            w_ne[k] = wne
            w_nw[k] = wnw
            sw, se = west(wne), east(wnw)
            if k < top:
                w_s[k + 1] = wn
                w_sw[k + 1] = sw
                w_se[k + 1] = se
            else:
                w_s[0] = from_below(wn)
                w_sw[0] = from_below(sw)
                w_se[0] = from_below(se)
            open_sum = (
                e_now
                + west(e_now)
                + n_now
                + n_prev
                + ne_now
                + west(ne_prev)
                + nw_now
                + east(nw_prev)
            )
            diag[k] = field(1, k) + ocean * open_sum + (1.0 - ocean)
            n_prev, ne_prev, nw_prev = n_now, ne_now, nw_now
            res_ref[k] = ocean * field(0, k)
            for ref in (r_mid, y_mid, z_mid, sol_ref, s_mid):
                ref[k] = zero
            z_pair[1, k] = zero
            k_pair[1, k] = zero

        def surface(k):
            return field(1, k) + (1.0 - field(FIELDS, k))

        low = surface(0) + w_s[0]
        high = surface(top) + w_n[top]
        for k in range(half):
            up, j = k, top - k
            g_low = 1.0 / (low + w_n[up])
            g_high = 1.0 / (high + w_s[j])
            f_g[up] = g_low
            f_g[j] = g_high
            if k < half - 1:
                f_a[up + 1] = w_n[up] * g_low
                f_a[j - 1] = w_s[j] * g_high
                low = surface(up + 1) + w_n[up] * (low * g_low)
                high = surface(j - 1) + w_s[j] * (high * g_high)
        mid = w_n[half - 1]
        inv_det = 1.0 / (low * high + mid * (low + high))
        mid_ll = (high + mid) * inv_det
        mid_lh = mid * inv_det
        mid_hh = (low + mid) * inv_det

        def line(read, out, u_ref):
            y, z = read(0), read(top)
            u_ref[0] = y
            u_ref[top] = z
            for k in range(1, half):
                j = top - k
                y = read(k) + f_a[k] * y
                z = read(j) + f_a[j] * z
                u_ref[k] = y
                u_ref[j] = z
            x = mid_ll * y + mid_lh * z
            v = mid_lh * y + mid_hh * z
            out[half - 1] = x
            out[half] = v
            for k in range(half - 2, -1, -1):
                j = top - k
                x = f_g[k] * u_ref[k] + f_a[k + 1] * x
                v = f_g[j] * u_ref[j] + f_a[j - 1] * v
                out[k] = x
                out[j] = v

        line(lambda k: w_s[0] if k == 0 else zero, resp0, y_ref)
        line(lambda k: w_n[top] if k == top else zero, resp1, y_ref)

        a, b, c, d = resp0[0], resp1[0], resp0[top], resp1[top]
        plan = []
        stride = 1
        while stride < SUB:
            cb, db = pltpu.roll(c, stride, 0), pltpu.roll(d, stride, 0)
            aa, ba = pltpu.roll(a, SUB - stride, 0), pltpu.roll(b, SUB - stride, 0)
            m00, m01 = 1.0 - a * db, -b * aa
            m10, m11 = -c * db, 1.0 - d * aa
            inv = 1.0 / (m00 * m11 - m01 * m10)
            i00, i01, i10, i11 = m11 * inv, -m01 * inv, -m10 * inv, m00 * inv
            t0, t1 = i00 * a + i01 * c, i00 * b + i01 * d
            t2, t3 = i10 * a + i11 * c, i10 * b + i11 * d
            plan.append((stride, i00, i01, i10, i11, t0, t1, t2, t3))
            a, b, c, d = t0 * cb, t1 * ba, t2 * cb, t3 * ba
            stride *= 2

        def interface(p, q):
            for stride, i00, i01, i10, i11, t0, t1, t2, t3 in plan:
                qb = pltpu.roll(q, stride, 0)
                pa = pltpu.roll(p, SUB - stride, 0)
                p, q = (
                    (i00 * p + i01 * q) + (t0 * qb + t1 * pa),
                    (i10 * p + i11 * q) + (t2 * qb + t3 * pa),
                )
            return from_below(q), from_above(p)

        def solve(read, u_ref):
            line(read, u_ref, u_ref)
            below, over = interface(u_ref[0], u_ref[top])

            def finish(k):
                value = u_ref[k] + below * resp0[k] + over * resp1[k]
                u_ref[k] = value
                return value

            return finish

        def walk(finish):
            last = finish(top)
            first = finish(0)
            last = (last, east(last), west(last))
            first = (first, east(first), west(first))
            prev = tuple(from_below(x) for x in last)
            now = first
            for k in range(depth):
                if k < top - 1:
                    value = finish(k + 1)
                    nxt = (value, east(value), west(value))
                elif k == top - 1:
                    nxt = last
                else:
                    nxt = tuple(from_above(x) for x in first)
                yield k, prev, now, nxt
                prev, now = now, nxt

        def column_sum(x):
            return jnp.sum(x, axis=0, keepdims=True)

        lane = iota((1, width), 1)
        relative = lax.rem(lane - odd * own + width, width)
        own_row = relative < own

        unit = jnp.where(is_top, 1.0, 0.0)
        h_mid, h_east = zero, zero
        for k, prev, now, nxt in walk(solve(lambda k: unit if k == top else zero, top_resp)):
            middle = diag[k] * now[0] - w_n[k] * nxt[0] - w_s[k] * prev[0]
            eastern = -(w_e[k] * now[1] + w_ne[k] * nxt[1] + w_se[k] * prev[1])
            c_mid[k] = middle
            c_east[k] = eastern
            c_west[k] = -(w_w[k] * now[2] + w_nw[k] * nxt[2] + w_sw[k] * prev[2])
            h_mid = h_mid + now[0] * middle
            h_east = h_east + now[0] * eastern

        def both(native_row, other_row):
            return jnp.where(own_row, native_row, pltpu.roll(other_row, own, 1))

        def last_row(x):
            return x[SUB - 1 :]

        stat_msg[0] = both(last_row(top_resp[top]), column_sum(h_mid))
        stat_msg[1] = both(column_sum(h_east), last_row(field(3, top)))
        stat_msg[2] = both(last_row(field(FIELDS, top)), jnp.zeros((1, width), jnp.float32))
        stat_recv[me] = stat_msg[...]

        def stat_start(place):
            pltpu.make_async_remote_copy(
                src_ref=stat_msg,
                dst_ref=stat_recv.at[me],
                send_sem=stat_send,
                recv_sem=stat_arrive,
                device_id=place,
                device_id_type=MESH,
            ).start()

        to_owners(stat_start)

        def send_rows(parity):
            def start(place):
                pltpu.make_async_remote_copy(
                    src_ref=msg.at[parity],
                    dst_ref=recv.at[parity, me],
                    send_sem=send_sem.at[parity],
                    recv_sem=recv_sem.at[parity],
                    device_id=place,
                    device_id_type=MESH,
                ).start()

            to_owners(start)

        def wait_for(every, sent, arrived):
            pltpu.make_async_remote_copy(
                src_ref=every,
                dst_ref=every,
                send_sem=sent,
                recv_sem=arrived,
                device_id=next_place,
                device_id_type=MESH,
            ).wait()

        lanes = iota((lon_count, width), 1)
        rows_id = iota((lon_count, width), 0)

        def assemble(read):
            lefts, rights = [], []
            for block in range(lon_count):
                spot = 2 * (block % 2) * pairs + block // 2
                lefts.append(read(spot))
                rights.append(read(spot + pairs))
            lefts = jnp.concatenate(lefts, axis=0)
            rights = jnp.concatenate(rights, axis=0)
            native_rows = jnp.where(lanes < own, lefts, rights)
            other_rows = pltpu.roll(jnp.where(lanes < own, rights, lefts), own, 1)
            return native_rows, other_rows

        total_cols = lon_count * width
        turn = lax.rem(map_buf[0] + lon * width, total_cols)
        back = total_cols - 1 - turn
        row_shift = back // width
        lane_shift = lax.rem(back, width)
        turn_index = width - 1 - lax.rem(lanes + lane_shift, width)

        def facing(x):
            flipped = jnp.concatenate(
                [x[b : b + 1] for b in range(lon_count - 1, -1, -1)], axis=0
            )
            moved = jnp.take_along_axis(flipped, turn_index, axis=1)
            first = pltpu.roll(moved, lax.rem(lon_count - row_shift, lon_count), 0)
            second = pltpu.roll(moved, lon_count - 1 - row_shift, 0)
            return jnp.where(lanes + lane_shift < width, first, second)

        block_row = 2 * pair + lat // 2
        odd_home = jnp.where(lanes < own // 2, 1, 0)
        even_home = jnp.where(lanes >= width - own // 2, -1, 0)
        home = block_row + odd * odd_home + (1 - odd) * even_home
        pick = rows_id == lax.rem(home + lon_count, lon_count)

        def window(x):
            return jnp.sum(jnp.where(pick, x, 0.0), axis=0, keepdims=True)

        def spread(x):
            return jnp.broadcast_to(x, (SUB, width))

        def total(x):
            return jnp.sum(x, keepdims=True)

        def advance(side, length, ratio, length2, ratio2, turned_row):
            g1, q1 = spread(ratio * length), spread(1.0 - ratio)
            g2, q2 = spread(ratio2 * length2), spread(1.0 - ratio2)
            rho, rho2 = spread(ratio), spread(ratio2)
            phi = spread(turned_row)
            for k in range(depth):
                z = z_pair[side, k]
                image = k_pair[side, k] - top_resp[k] * phi
                old, older = sol_ref[k], s_mid[k]
                toward = rho * z - g1 * image + q1 * z_mid[k]
                between_sol = rho * old + g1 * z + q1 * older
                z_mid[k] = toward
                s_mid[k] = between_sol
                sol_ref[k] = rho2 * between_sol + g2 * toward + q2 * old

        def block_step(step, carry):
            length_old, ratio_old, mu_old, nu_old, length_mid, ratio_mid, phi_old = carry
            parity = lax.rem(step, 2)
            z_ref, k_ref = z_pair.at[parity], k_pair.at[parity]
            acc = [zero] * 9

            def stencil(k, prev, now, nxt):
                return (
                    (diag[k] * now[0] - w_e[k] * now[1] - w_w[k] * now[2])
                    - (w_n[k] * nxt[0] + w_ne[k] * nxt[1] + w_nw[k] * nxt[2])
                    - (w_s[k] * prev[0] + w_se[k] * prev[1] + w_sw[k] * prev[2])
                )

            for k, prev, now, nxt in walk(solve(lambda k: res_ref[k], z_ref)):
                value = stencil(k, prev, now, nxt)
                y_ref[k] = value
                acc[k % 2] = acc[k % 2] + res_ref[k] * now[0]
                acc[2 + k % 2] = acc[2 + k % 2] + now[0] * value
            for k, prev, now, nxt in walk(solve(lambda k: y_ref[k], k_ref)):
                value = stencil(k, prev, now, nxt)
                w_ref[k] = value
                acc[4 + k % 2] = acc[4 + k % 2] + y_ref[k] * now[0]
                acc[6 + k % 2] = acc[6 + k % 2] + now[0] * value
                acc[8] = acc[8] + top_resp[k] * value
            parts = [
                total(jnp.where(own_row, acc[2 * i] + acc[2 * i + 1], 0.0)) for i in range(4)
            ]
            sums = jnp.zeros((1, width), jnp.float32)
            for i in range(4):
                sums = jnp.where(relative == own + i, parts[i], sums)
            msg[parity, 0] = both(last_row(z_ref[top]), last_row(k_ref[top]))
            msg[parity, 1] = jnp.where(own_row, column_sum(acc[8]), sums)
            recv[parity, me] = msg[parity]
            send_rows(parity)
            advance(1 - parity, length_mid, ratio_mid, length_old, ratio_old, phi_old)

            @pl.when(step == 0)
            def _():
                wait_for(stat_recv.at[0 : n_own - 1], stat_send, stat_arrive)
                h0, h1 = assemble(lambda spot: stat_recv[spot, 0])
                h2, north = assemble(lambda spot: stat_recv[spot, 1])
                ocean, _unused = assemble(lambda spot: stat_recv[spot, 2])
                fold_open = 0.5 * (north + facing(north))
                fold_own = fold_open * ocean
                fold_far = fold_own * facing(ocean)
                for i, x in enumerate(
                    (h0, h1, 2.0 * h2, fold_own, fold_far, facing(h0), facing(fold_own))
                ):
                    whole[i] = x

            wait_for(recv.at[parity, 0 : n_own - 1], send_sem.at[parity], recv_sem.at[parity])
            tau0, tau1 = assemble(lambda spot: recv[parity, spot, 0])
            tail, rest_rows = assemble(lambda spot: recv[parity, spot, 1])
            h0, h1, h2, fold_own, fold_far, h0_facing, own_facing = (whole[i] for i in range(7))
            tau0_facing, tau1_facing = facing(tau0), facing(tau1)
            phi0 = fold_far * tau0_facing - fold_own * tau0
            phi0_facing = fold_far * tau0 - own_facing * tau0_facing
            top1 = tau1 - h0 * phi0
            phi1 = fold_far * (tau1_facing - h0_facing * phi0_facing) - fold_own * top1
            shifted = east(phi0)
            shifted = jnp.where(
                lanes == width - 1, pltpu.roll(shifted, lon_count - 1, 0), shifted
            )
            rest_lane = lax.rem(lanes, own)

            def moment(i, x):
                return total(jnp.where(rest_lane == i, rest_rows, 0.0) + x)

            m0 = moment(0, 0.0)
            m1 = moment(1, -tau0 * phi0)
            m2 = moment(2, phi0 * (h0 * phi0 - 2.0 * tau1))
            m3 = moment(3, phi0 * (h1 * phi0 + h2 * shifted - 2.0 * tail) - top1 * phi1)
            phi0_row, phi1_row = window(phi0), window(phi1)

            start = step == 0
            length = m0 / m1
            factor = ratio_old * length_old
            ratio = jnp.where(start, 1.0, 1.0 / (1.0 - (length * m0) / (factor * mu_old)))
            cross = jnp.where(start, 0.0, -m0 / factor)
            cross2 = jnp.where(start, 0.0, (ratio_old * cross - m1) / factor)
            q = 1.0 - ratio
            gain = ratio * length
            mu = (
                gain * gain * m2
                - ratio * ratio * m0
                + q * q * mu_old
                - 2.0 * gain * q * cross
            )
            nu = (
                ratio * ratio * m1
                + gain * gain * m3
                + q * q * nu_old
                - 2.0 * ratio * gain * m2
                + 2.0 * ratio * q * cross
                - 2.0 * gain * q * cross2
            )
            length2 = mu / nu
            ratio2 = 1.0 / (1.0 - (length2 * mu) / (gain * m0))
            rho, g1, q1 = spread(ratio), spread(gain), spread(q)
            rho2, g2, q2 = spread(ratio2), spread(ratio2 * length2), spread(1.0 - ratio2)
            p_mid, p_east, p_west = (
                spread(phi0_row),
                spread(east(phi0_row)),
                spread(west(phi0_row)),
            )
            phi1_top = jnp.where(is_top, spread(phi1_row), 0.0)
            phi0_top = jnp.where(is_top, p_mid, 0.0)
            for k in range(depth):
                image = y_ref[k]
                second = w_ref[k] - (c_mid[k] * p_mid + c_east[k] * p_east + c_west[k] * p_west)
                if k == top:
                    image = image - phi0_top
                    second = second - phi1_top
                res = res_ref[k]
                between_res = rho * res - g1 * image + q1 * r_mid[k]
                toward = rho * image - g1 * second + q1 * y_mid[k]
                r_mid[k] = between_res
                y_mid[k] = toward
                res_ref[k] = rho2 * between_res - g2 * toward + q2 * res
            return (length2, ratio2, mu, nu, length, ratio, phi0_row)

        one = jnp.ones((1, 1), jnp.float32)
        nil = jnp.zeros((1, 1), jnp.float32)
        carry = (nil, one, one, one, nil, one, jnp.zeros((1, width), jnp.float32))
        carry = lax.fori_loop(0, ITERS // 2, block_step, carry)
        length2, ratio2, _, _, length, ratio, phi_row = carry
        advance((ITERS // 2 - 1) % 2, length, ratio, length2, ratio2, phi_row)

        for k in range(depth):
            value = jnp.where(own_row, sol_ref[k], pltpu.roll(res_ref[k], own, 1))
            back_msg[pl.ds(k, SUB, stride=depth), :] = value

        for a in range(lat_count):

            @pl.when(jnp.logical_or(lat != a, lat < 2))
            def _(a=a):
                back_copy(a).start()

        @pl.when(lat >= 2)
        def _():
            back_recv[odd] = back_msg[pl.ds(pl.multiple_of(lat * rows, rows), rows), :]

        for a in range(lat_count):

            @pl.when(jnp.logical_or(lat != a, lat < 2))
            def _(a=a):
                back_copy(a).wait_send()

    pl.when(is_owner)(solve_columns)

    for copy, stays in outgoing:
        if stays is None:
            copy.wait_send()
        else:
            pl.when(jnp.logical_not(stays))(copy.wait_send)

    for side in range(2):

        @pl.when(jnp.logical_or(core == 0, lat != 2 + side))
        def _(side=side):
            pltpu.make_async_remote_copy(
                src_ref=back_msg.at[0:rows],
                dst_ref=back_recv.at[side],
                send_sem=back_send.at[0],
                recv_sem=back_arrive.at[side],
                device_id=left_place,
                device_id_type=MESH,
            ).wait_recv()

    for v in range(rows // SUB):
        sl = slice(v * SUB, (v + 1) * SUB)
        first, second = back_recv[0, sl], back_recv[1, sl]
        sol_out[sl] = jnp.where(wide < own, first, second)
        res_out[sl] = pltpu.roll(jnp.where(wide < own, second, first), own, 1)


def shards(
    right_side,
    surface_term,
    east_coupling,
    north_coupling,
    neast_coupling,
    nwest_coupling,
    land_sea,
    fold_map,
):
    rows, width = right_side.shape
    lat_count = lax.axis_size("lat")
    lon_count = lax.axis_size("lon")
    n_own = lat_count * lon_count // 2
    depth = rows * lat_count // SUB
    subs = SUB // lat_count
    assert lat_count == 4 and ITERS % 2 == 0
    band = subs * (FIELDS // 2 * depth + depth // 2)
    thin = subs * depth // 2

    block = pltpu.VMEM((depth, SUB, width), jnp.float32)
    answer = jax.ShapeDtypeStruct((rows, width), jnp.float32)
    vmem = pl.BlockSpec(memory_space=pltpu.VMEM)
    dma = pltpu.SemaphoreType.DMA

    def held(*shape):
        return pltpu.VMEM((*shape, width), jnp.float32)

    return pl.pallas_call(
        functools.partial(kernel, lat_count, lon_count),
        out_shape=(answer, answer),
        in_specs=[pl.BlockSpec(memory_space=pl.ANY)] * 8,
        out_specs=(vmem, vmem),
        scratch_shapes=[block] * 25
        + [
            held(2, depth, SUB),
            held(2, depth, SUB),
            held(FIELDS, depth, SUB),
            held(FIELDS, rows),
            pltpu.VMEM((rows, width), jnp.int32),
            pltpu.SMEM((width,), jnp.int32),
            held(2, band),
            held(2, thin),
            held(lat_count * band),
            held(lat_count * thin),
            held(3, 1),
            held(n_own, 3, 1),
            held(7, lon_count),
            held(2, 2, 1),
            held(2, n_own, 2, 1),
            held(lat_count * rows),
            held(2, rows),
            dma((FIELDS + 2,)),
            dma((2,)),
            dma((lat_count,)),
            dma((2,)),
            dma((lat_count,)),
            dma(()),
            dma(()),
            dma((2,)),
            dma((2,)),
            dma((lat_count,)),
            dma((2,)),
        ],
        compiler_params=pltpu.CompilerParams(collective_id=0, has_side_effects=True),
    )(
        right_side,
        surface_term,
        east_coupling,
        north_coupling,
        neast_coupling,
        nwest_coupling,
        land_sea,
        fold_map,
    )


def solution(mesh):
    return jax.shard_map(
        shards,
        mesh=mesh,
        in_specs=(P("lat", "lon"),) * 7 + (P("lon"),),
        out_specs=(P("lat", "lon"), P("lat", "lon")),
        check_vma=False,
    )
```

profile of v0, /device:TPU:0, one launch (start us, length us, event | category | flops | bytes accessed | tf_op | source)
XLA Modules:
  0.0 45.1 jit_solution(2975360886942747316)
XLA Ops:
  0.6 42.3 %shard_map.95 = (f32[128,128]{1,0:T(8,128)}, f32[128,128]{1,0:T(8,128)}) custom-call(f32[128,128]{1,0:T(8,128)} %right_ref.1, f32[128,128]{1,0:T(8,128)} %surface_ref.1, f32[128,128]{1,0:T(8,128)} %east_ref.1, f32[128,128]{1,0:T(8,128)} %north_ref.1, f32[128,128]{1,0:T(8,128)} %neast_ref.1, f32[128,128]{1,0:T(8,128)} %nwest_ref.1, s32[128,128]{1,0:T(8,128)} %land_ref.1, ...), custom_call_target="tpu_custom_call" | custom-call | tf_op jit(solution)/shard_map/pallas_call | solution.py:832
  43.0 0.0 copy-start
  43.0 1.5 %copy.12 = f32[128,128]{1,0:T(8,128)} copy(f32[128,128]{1,0:T(8,128)} %get-tuple-element.4) | data formatting | bytes 131072
  44.5 0.0 copy-done
  44.5 0.6 %copy.13 = f32[128,128]{1,0:T(8,128)} copy(f32[128,128]{1,0:T(8,128)S(1)} %copy-done) | data formatting | bytes 131072
Async XLA Ops:
  43.0 1.5 %copy-start = (f32[128,128]{1,0:T(8,128)S(1)}, f32[128,128]{1,0:T(8,128)}, u32[]{:S(2)}) copy-start(f32[128,128]{1,0:T(8,128)} %get-tuple-element.5) | copy-start | bytes 196612
where the time goes:
time: 45.7 us; the launch traced here: 45.1 us
  Pallas kernels  42.3 us (93%)
  local copies, waits for them, and re-layouts  2.14 us (5%)
  between operations  0.65 us (1%)
    pallas_call x1, Pallas kernels, shards(): pl.pallas_call(functools.partial(kernel, lat_count, lon_count), out_shape...  42.3 us
    unnamed x4, local copies, waits for them, and re-layouts  2.14 us

commit v1 on v0

v1 whole, which is shorter than its diff:
```python
import functools

import jax
import jax.numpy as jnp
from jax import lax
from jax.experimental import pallas as pl
from jax.experimental.pallas import tpu as pltpu
from jax.sharding import PartitionSpec as P

ITERS = 8
SUB = 8
FIELDS = 6
MESH = pl.DeviceIdType.MESH


def iota(shape, dim):
    return lax.broadcasted_iota(jnp.int32, shape, dim)


def east(x):
    return pltpu.roll(x, x.shape[-1] - 1, x.ndim - 1)


def west(x):
    return pltpu.roll(x, 1, x.ndim - 1)


def from_above(x):
    return pltpu.roll(x, SUB - 1, 0)


def from_below(x):
    return pltpu.roll(x, 1, 0)


def alternate(size):
    ring = []
    for i in range(1, size // 2 + 1):
        ring += [size - i, i]
    return list(dict.fromkeys([*ring, 0]))


def kernel(
    lat_count,
    lon_count,
    right_ref,
    surface_ref,
    east_ref,
    north_ref,
    neast_ref,
    nwest_ref,
    land_ref,
    map_ref,
    sol_out,
    res_out,
    w_e,
    w_w,
    w_n,
    w_s,
    w_ne,
    w_sw,
    w_nw,
    w_se,
    diag,
    f_a,
    f_g,
    resp0,
    resp1,
    top_resp,
    c_mid,
    c_east,
    c_west,
    res_ref,
    basis,
    images,
    surf,
    o_mid,
    o_east,
    o_west,
    n_raw,
    g_east,
    g_west,
    given,
    land_buf,
    map_buf,
    big_msg,
    small_msg,
    big_recv,
    small_recv,
    stat_msg,
    stat_recv,
    msg,
    recv,
    back_msg,
    back_recv,
    in_sem,
    big_send,
    big_arrive,
    small_send,
    small_arrive,
    stat_send,
    stat_arrive,
    send_sem,
    recv_sem,
    back_send,
    back_arrive,
):
    pairs = lon_count // 2
    n_own = lat_count * pairs
    lat = lax.axis_index("lat")
    lon = lax.axis_index("lon")
    pair = lon // 2
    core = lax.rem(lon, 2)
    me = lat * pairs + pair
    depth, _, width = res_ref.shape
    rows = depth * SUB // lat_count
    subs = SUB // lat_count
    halo = ITERS
    own = 2 * width // lat_count
    big = own + halo
    rest = width - big
    band = big_msg.shape[2]
    thin = small_msg.shape[2]
    seg = band // subs
    half = depth // 2
    top = depth - 1
    odd = lax.rem(lat, 2)
    is_owner = core == 1

    lats = [lax.rem(lat + d, lat_count) for d in range(lat_count)]
    owners = [2 * lax.rem(pair + d, pairs) + 1 for d in range(pairs)]
    few = n_own <= 64
    peers = [(p, q) for q in alternate(pairs) for p in alternate(lat_count) if p or q]

    def to_owners(act):
        if few:
            for p, q in peers:
                act((lats[p], owners[q]))
            return

        def one(step, carry):
            peer = lax.rem(me + step, n_own)
            act((peer // pairs, 2 * lax.rem(peer, pairs) + 1))
            return carry

        lax.fori_loop(1, n_own, one, 0)

    left_place = (2 * core, 2 * pair + 1)
    right_place = (2 * core + 1, 2 * pair + 1)
    next_place = (lax.rem(2 * core + 2, lat_count), 2 * lax.rem(pair + core, pairs) + 1)
    back_pair = lax.rem(pair + core + pairs - 1, pairs)
    prev_place = (lax.rem(2 * core + 3, lat_count), 2 * back_pair + 1)

    barrier = pltpu.get_barrier_semaphore()

    def greet(place):
        pl.semaphore_signal(barrier, inc=1, device_id=place, device_id_type=MESH)

    @pl.when(is_owner)
    def _():
        to_owners(greet)
        last_lat = jnp.where(lat == lat_count - 1, 1, 0)
        plain = 2 * lax.rem(pair + last_lat, pairs)
        for a in range(lat_count):
            greet((a, plain))

    @pl.when(core == 0)
    def _():
        for place in (left_place, right_place, next_place, prev_place):
            greet(place)

    sources = (surface_ref, north_ref, right_ref, east_ref, neast_ref, nwest_ref)
    loads = [
        pltpu.make_async_copy(ref, given.at[i], in_sem.at[i]) for i, ref in enumerate(sources)
    ]
    land_load = pltpu.make_async_copy(land_ref, land_buf, in_sem.at[FIELDS])
    map_load = pltpu.make_async_copy(map_ref, map_buf, in_sem.at[FIELDS + 1])
    land_load.start()
    for copy in loads:
        copy.start()
    map_load.start()

    wide = iota((SUB, width), 1)
    zero = jnp.zeros((SUB, width), jnp.float32)
    sixteenth = wide // halo
    groups = width // halo
    here_big = pl.ds(pl.multiple_of(lat * band, SUB), band)
    here_thin = pl.ds(pl.multiple_of(lat * thin, SUB), thin)

    def big_copy(side, c):
        return pltpu.make_async_remote_copy(
            src_ref=big_msg.at[side, c],
            dst_ref=big_recv.at[c, here_big],
            send_sem=big_send.at[side, c],
            recv_sem=big_arrive.at[c, lat],
            device_id=(left_place, right_place)[side],
            device_id_type=MESH,
        )

    def thin_copy(side, c):
        return pltpu.make_async_remote_copy(
            src_ref=small_msg.at[side, c],
            dst_ref=small_recv.at[c, here_thin],
            send_sem=small_send.at[side, c],
            recv_sem=small_arrive.at[c, lat],
            device_id=(next_place, prev_place)[side],
            device_id_type=MESH,
        )

    big_stays = [jnp.logical_and(is_owner, lat == 2 + side) for side in range(2)]
    thin_stays = jnp.logical_and(is_owner, lat == 1)

    def pack(c):
        for s in range(subs):
            for v in range(depth // SUB):
                sl = slice(s * depth + v * SUB, s * depth + (v + 1) * SUB)
                first, second = given[2 * c, sl], given[2 * c + 1, sl]
                second = pltpu.roll(second, own, 1)
                at = s * seg + v * SUB
                to = slice(at, at + SUB)
                big_msg[0, c, to] = jnp.where(wide < big, first, second)
                big_msg[1, c, to] = jnp.where(wide >= rest, first, second)
            acc_l, acc_r, acc_n, acc_p = zero, zero, zero, zero
            for j in range(SUB):
                phase = pl.ds(s * depth + j, SUB, stride=SUB)
                first, second = given[2 * c, phase, :], given[2 * c + 1, phase, :]
                lane = halo * j
                even_b = pltpu.roll(second, (lane + own) % width, 1)
                odd_b = pltpu.roll(second, lane + halo, 1)
                even_a = pltpu.roll(first, lane, 1) if lane else first
                odd_a = pltpu.roll(first, (lane + own + halo) % width, 1)
                hit = lax.rem(sixteenth, groups // 2) == j
                acc_l = jnp.where(hit, even_b, acc_l)
                acc_r = jnp.where(hit, odd_b, acc_r)
                acc_n = jnp.where(sixteenth == (j + groups - 1) % groups, even_a, acc_n)
                acc_n = jnp.where(sixteenth == (j + groups // 2 - 1) % groups, even_b, acc_n)
                acc_p = jnp.where(sixteenth == (j + groups // 2 + 1) % groups, odd_a, acc_p)
                acc_p = jnp.where(sixteenth == (j + 1) % groups, odd_b, acc_p)
            at = s * seg + depth
            big_msg[0, c, at : at + SUB] = acc_l
            big_msg[1, c, at : at + SUB] = acc_r
            at = s * SUB
            small_msg[0, c, at : at + SUB] = acc_n
            small_msg[1, c, at : at + SUB] = acc_p

    def send(c):
        for side in range(2):
            pl.when(jnp.logical_not(big_stays[side]))(big_copy(side, c).start)

            @pl.when(big_stays[side])
            def _(side=side):
                pltpu.make_async_copy(
                    big_msg.at[side, c], big_recv.at[c, here_big], big_arrive.at[c, lat]
                ).start()

        thin_copy(0, c).start()
        pl.when(jnp.logical_not(thin_stays))(thin_copy(1, c).start)

        @pl.when(thin_stays)
        def _():
            pltpu.make_async_copy(
                small_msg.at[1, c], small_recv.at[c, here_thin], small_arrive.at[c, lat]
            ).start()

    land_load.wait()
    for c in range(FIELDS // 2):
        loads[2 * c].wait()
        loads[2 * c + 1].wait()
        if c == 0:
            for v in range(rows // SUB):
                sl = slice(v * SUB, (v + 1) * SUB)
                given[0, sl] = given[0, sl] * land_buf[sl].astype(jnp.float32)
        pack(c)
        if c == 0:

            @pl.when(is_owner)
            def _():
                pl.semaphore_wait(barrier, n_own - 1 + lat_count)

            @pl.when(core == 0)
            def _():
                pl.semaphore_wait(barrier, lat_count)

        send(c)
    map_load.wait()

    def back_copy(a):
        return pltpu.make_async_remote_copy(
            src_ref=back_msg.at[a * rows : (a + 1) * rows],
            dst_ref=back_recv.at[odd],
            send_sem=back_send.at[a],
            recv_sem=back_arrive.at[odd],
            device_id=(a, 2 * pair + lat // 2),
            device_id_type=MESH,
        )

    def solve_columns():
        def receive(c):
            for a in range(lat_count):
                pltpu.make_async_remote_copy(
                    src_ref=big_msg.at[0, c],
                    dst_ref=big_recv.at[c, a * band : (a + 1) * band],
                    send_sem=big_send.at[0, c],
                    recv_sem=big_arrive.at[c, a],
                    device_id=left_place,
                    device_id_type=MESH,
                ).wait_recv()
                pltpu.make_async_remote_copy(
                    src_ref=small_msg.at[0, c],
                    dst_ref=small_recv.at[c, a * thin : (a + 1) * thin],
                    send_sem=small_send.at[0, c],
                    recv_sem=small_arrive.at[c, a],
                    device_id=next_place,
                    device_id_type=MESH,
                ).wait_recv()

        def between(low, size):
            return (wide >= low) & (wide < low + size)

        native = between(odd * rest, big)
        side = between((1 - odd) * (width - halo), halo)
        ends = between(own - halo, 2 * halo) | between(odd * (width - halo), halo)
        strip_hit = [
            lax.rem(sixteenth, groups // 2) == lax.rem(j + groups // 2 - 1 + 2 * odd, groups // 2)
            for j in range(SUB)
        ]
        shifts = [lax.rem(odd * rest - halo * j + width, width) for j in range(SUB)]

        def unpack(c, k):
            j = k % SUB
            strip = small_recv[c, pl.ds(k // SUB, SUB, stride=SUB), :]
            spill = big_recv[c, pl.ds(depth + k // SUB, SUB, stride=seg), :]
            packed = big_recv[c, pl.ds(k, SUB, stride=seg), :]
            moved = pltpu.roll(jnp.where(strip_hit[j], strip, spill), shifts[j], 1)
            first = jnp.where(native, packed, jnp.where(side, moved, 0.0))
            second = jnp.where(native, jnp.where(ends, moved, 0.0), packed)
            return first, pltpu.roll(second, own, 1)

        is_top = iota((SUB, width), 0) == SUB - 1

        def shut(value, k):
            return jnp.where(is_top, 0.0, value) if k == top else value

        def is_ocean(surface):
            return jnp.where(surface > 0.0, 1.0, 0.0)

        receive(0)
        below_north = None
        for k in range(depth):
            surface, north = unpack(0, k)
            ocean = is_ocean(surface)
            surf[k] = surface
            o_mid[k] = ocean
            o_east[k] = east(ocean)
            o_west[k] = west(ocean)
            n_raw[k] = north
            if k:
                wn = below_north * ocean
                w_n[k - 1] = wn
                w_s[k] = wn
            below_north = shut(north, k) * ocean
        wn = below_north * from_above(o_mid[0])
        w_n[top] = wn
        w_s[0] = from_below(wn)

        def line_surface(k):
            return surf[k] + (1.0 - o_mid[k])

        low = line_surface(0) + w_s[0]
        high = line_surface(top) + w_n[top]
        for k in range(half):
            up, j = k, top - k
            g_low = 1.0 / (low + w_n[up])
            g_high = 1.0 / (high + w_s[j])
            f_g[up] = g_low
            f_g[j] = g_high
            if k < half - 1:
                f_a[up + 1] = w_n[up] * g_low
                f_a[j - 1] = w_s[j] * g_high
                low = line_surface(up + 1) + w_n[up] * (low * g_low)
                high = line_surface(j - 1) + w_s[j] * (high * g_high)
        mid = w_n[half - 1]
        inv_det = 1.0 / (low * high + mid * (low + high))
        mid_ll = (high + mid) * inv_det
        mid_lh = mid * inv_det
        mid_hh = (low + mid) * inv_det

        def line(read, out, u_ref):
            y, z = read(0), read(top)
            u_ref[0] = y
            u_ref[top] = z
            for k in range(1, half):
                j = top - k
                y = read(k) + f_a[k] * y
                z = read(j) + f_a[j] * z
                u_ref[k] = y
                u_ref[j] = z
            x = mid_ll * y + mid_lh * z
            v = mid_lh * y + mid_hh * z
            out[half - 1] = x
            out[half] = v
            for k in range(half - 2, -1, -1):
                j = top - k
                x = f_g[k] * u_ref[k] + f_a[k + 1] * x
                v = f_g[j] * u_ref[j] + f_a[j - 1] * v
                out[k] = x
                out[j] = v

        line(lambda k: w_s[0] if k == 0 else zero, resp0, images.at[0])
        line(lambda k: w_n[top] if k == top else zero, resp1, images.at[0])

        a, b, c, d = resp0[0], resp1[0], resp0[top], resp1[top]
        plan = []
        stride = 1
        while stride < SUB:
            cb, db = pltpu.roll(c, stride, 0), pltpu.roll(d, stride, 0)
            aa, ba = pltpu.roll(a, SUB - stride, 0), pltpu.roll(b, SUB - stride, 0)
            m00, m01 = 1.0 - a * db, -b * aa
            m10, m11 = -c * db, 1.0 - d * aa
            inv = 1.0 / (m00 * m11 - m01 * m10)
            i00, i01, i10, i11 = m11 * inv, -m01 * inv, -m10 * inv, m00 * inv
            t0, t1 = i00 * a + i01 * c, i00 * b + i01 * d
            t2, t3 = i10 * a + i11 * c, i10 * b + i11 * d
            plan.append((stride, i00, i01, i10, i11, t0, t1, t2, t3))
            a, b, c, d = t0 * cb, t1 * ba, t2 * cb, t3 * ba
            stride *= 2

        def interface(p, q):
            for stride, i00, i01, i10, i11, t0, t1, t2, t3 in plan:
                qb = pltpu.roll(q, stride, 0)
                pa = pltpu.roll(p, SUB - stride, 0)
                p, q = (
                    (i00 * p + i01 * q) + (t0 * qb + t1 * pa),
                    (i10 * p + i11 * q) + (t2 * qb + t3 * pa),
                )
            return from_below(q), from_above(p)

        def solve(read, u_ref):
            line(read, u_ref, u_ref)
            below, over = interface(u_ref[0], u_ref[top])

            def finish(k):
                value = u_ref[k] + below * resp0[k] + over * resp1[k]
                u_ref[k] = value
                return value

            return finish

        def walk(finish):
            last = finish(top)
            first = finish(0)
            last = (last, east(last), west(last))
            first = (first, east(first), west(first))
            prev = tuple(from_below(x) for x in last)
            now = first
            for k in range(depth):
                if k < top - 1:
                    value = finish(k + 1)
                    nxt = (value, east(value), west(value))
                elif k == top - 1:
                    nxt = last
                else:
                    nxt = tuple(from_above(x) for x in first)
                yield k, prev, now, nxt
                prev, now = now, nxt

        def column_sum(x):
            return jnp.sum(x, axis=0, keepdims=True)

        lane = iota((1, width), 1)
        relative = lax.rem(lane - odd * own + width, width)
        own_row = relative < own

        unit = jnp.where(is_top, 1.0, 0.0)
        finish = solve(lambda k: unit if k == top else zero, top_resp)
        for k in range(depth):
            value = finish(k)
            g_east[k] = east(value)
            g_west[k] = west(value)

        receive(1)
        n_prev = from_below(shut(n_raw[top], top))
        for k in range(depth):
            right, eastern = unpack(1, k)
            ocean = o_mid[k]
            inner = west(eastern)
            w_e[k] = eastern * ocean * o_east[k]
            w_w[k] = inner * ocean * o_west[k]
            n_now = shut(n_raw[k], k)
            diag[k] = eastern + inner + n_now + n_prev
            n_prev = n_now
            res_ref[k] = ocean * right

        receive(2)

        def corners(k):
            ne, nw = (shut(x, k) for x in unpack(2, k))
            ne_west, nw_east = west(ne), east(nw)
            if k < top:
                next_mid, next_east, next_west = o_mid[k + 1], o_east[k + 1], o_west[k + 1]
            else:
                next_mid, next_east, next_west = (
                    from_above(x[0]) for x in (o_mid, o_east, o_west)
                )
            ocean = o_mid[k]
            wne, wnw = ne * ocean * next_east, nw * ocean * next_west
            sw, se = ne_west * o_west[k] * next_mid, nw_east * o_east[k] * next_mid
            w_ne[k] = wne
            w_nw[k] = wnw
            return ne + nw, ne_west + nw_east, sw, se, wne, wnw

        last = corners(top)
        sum_prev, sw, se = (from_below(x) for x in (last[1], last[2], last[3]))
        h_mid, h_east = zero, zero
        for k in range(depth):
            now = corners(k) if k < top else last
            ocean = o_mid[k]
            value = surf[k] + ocean * (diag[k] + now[0] + sum_prev) + (1.0 - ocean)
            diag[k] = value
            w_sw[k] = sw
            w_se[k] = se
            around = (top_resp, g_east, g_west)
            prev = [x[k - 1] if k else from_below(x[top]) for x in around]
            nxt = [x[k + 1] if k < top else from_above(x[0]) for x in around]
            here = top_resp[k]
            middle = value * here - w_n[k] * nxt[0] - w_s[k] * prev[0]
            eastern = -(w_e[k] * g_east[k] + now[4] * nxt[1] + se * prev[1])
            c_mid[k] = middle
            c_east[k] = eastern
            c_west[k] = -(w_w[k] * g_west[k] + now[5] * nxt[2] + sw * prev[2])
            h_mid = h_mid + here * middle
            h_east = h_east + here * eastern
            sum_prev, sw, se = now[1], now[2], now[3]

        def both(native_row, other_row):
            return jnp.where(own_row, native_row, pltpu.roll(other_row, own, 1))

        def last_row(x):
            return x[SUB - 1 :]

        stat_msg[0] = both(last_row(top_resp[top]), column_sum(h_mid))
        stat_msg[1] = both(column_sum(h_east), last_row(n_raw[top]))
        stat_msg[2] = both(last_row(o_mid[top]), jnp.zeros((1, width), jnp.float32))
        stat_recv[me] = stat_msg[...]

        def stat_start(place):
            pltpu.make_async_remote_copy(
                src_ref=stat_msg,
                dst_ref=stat_recv.at[me],
                send_sem=stat_send,
                recv_sem=stat_arrive,
                device_id=place,
                device_id_type=MESH,
            ).start()

        to_owners(stat_start)

        def send_rows(b):
            def start(place):
                pltpu.make_async_remote_copy(
                    src_ref=msg.at[b],
                    dst_ref=recv.at[b, me],
                    send_sem=send_sem.at[b],
                    recv_sem=recv_sem.at[b],
                    device_id=place,
                    device_id_type=MESH,
                ).start()

            to_owners(start)

        def wait_for(every, sent, arrived):
            pltpu.make_async_remote_copy(
                src_ref=every,
                dst_ref=every,
                send_sem=sent,
                recv_sem=arrived,
                device_id=next_place,
                device_id_type=MESH,
            ).wait()

        lanes = iota((lon_count, width), 1)
        rows_id = iota((lon_count, width), 0)

        def assemble(read):
            lefts, rights = [], []
            for block in range(lon_count):
                spot = 2 * (block % 2) * pairs + block // 2
                lefts.append(read(spot))
                rights.append(read(spot + pairs))
            lefts = jnp.concatenate(lefts, axis=0)
            rights = jnp.concatenate(rights, axis=0)
            native_rows = jnp.where(lanes < own, lefts, rights)
            other_rows = pltpu.roll(jnp.where(lanes < own, rights, lefts), own, 1)
            return native_rows, other_rows

        total_cols = lon_count * width
        turn = lax.rem(map_buf[0] + lon * width, total_cols)
        back = total_cols - 1 - turn
        row_shift = back // width
        lane_shift = lax.rem(back, width)
        turn_index = width - 1 - lax.rem(lanes + lane_shift, width)

        def facing(x):
            flipped = jnp.concatenate(
                [x[b : b + 1] for b in range(lon_count - 1, -1, -1)], axis=0
            )
            moved = jnp.take_along_axis(flipped, turn_index, axis=1)
            first = pltpu.roll(moved, lax.rem(lon_count - row_shift, lon_count), 0)
            second = pltpu.roll(moved, lon_count - 1 - row_shift, 0)
            return jnp.where(lanes + lane_shift < width, first, second)

        block_row = 2 * pair + lat // 2
        odd_home = jnp.where(lanes < own // 2, 1, 0)
        even_home = jnp.where(lanes >= width - own // 2, -1, 0)
        home = block_row + odd * odd_home + (1 - odd) * even_home
        pick = rows_id == lax.rem(home + lon_count, lon_count)

        def window(x):
            return jnp.sum(jnp.where(pick, x, 0.0), axis=0, keepdims=True)

        def spread(x):
            return jnp.broadcast_to(x, (SUB, width))

        def total(x):
            return jnp.sum(x, keepdims=True)

        def east_whole(x):
            moved = east(x)
            return jnp.where(lanes == width - 1, pltpu.roll(moved, lon_count - 1, 0), moved)

        def west_whole(x):
            moved = west(x)
            return jnp.where(lanes == 0, pltpu.roll(moved, 1, 0), moved)

        def stencil(k, prev, now, nxt):
            return (
                (diag[k] * now[0] - w_e[k] * now[1] - w_w[k] * now[2])
                - (w_n[k] * nxt[0] + w_ne[k] * nxt[1] + w_nw[k] * nxt[2])
                - (w_s[k] * prev[0] + w_se[k] * prev[1] + w_sw[k] * prev[2])
            )

        def product(p, q):
            return [[p[i][0] * q[0][j] + p[i][1] * q[1][j] for j in (0, 1)] for i in (0, 1)]

        def turned_product(p, q):
            return [[p[0][i] * q[0][j] + p[1][i] * q[1][j] for j in (0, 1)] for i in (0, 1)]

        def plus(p, q):
            return [[p[i][j] + q[i][j] for j in (0, 1)] for i in (0, 1)]

        def minus(p, q):
            return [[p[i][j] - q[i][j] for j in (0, 1)] for i in (0, 1)]

        def factor(p):
            first = 1.0 / p[0][0]
            slope = p[0][1] * first
            return first, slope, 1.0 / (p[1][1] - slope * p[0][1]), p[0][1]

        def solve_pair(f, u, v):
            second = (v - f[1] * u) * f[2]
            return (u - f[3] * second) * f[0], second

        blocks = ITERS // 2
        factors, links, tails, phi_rows = [], {}, [], []
        weight_of = [[0.0, 0.0] for _ in range(blocks)]
        rest_lane = lax.rem(lane, own)
        for b in range(blocks):
            z_ref, k_ref = basis.at[2 * b], basis.at[2 * b + 1]
            y_ref, w_ref = images.at[2 * b], images.at[2 * b + 1]
            acc = [zero] * 9
            old = [zero] * (4 * b)
            for k, prev, now, nxt in walk(solve(lambda k: res_ref[k], z_ref)):
                value = stencil(k, prev, now, nxt)
                y_ref[k] = value
                acc[k % 2] = acc[k % 2] + res_ref[k] * now[0]
                acc[2 + k % 2] = acc[2 + k % 2] + now[0] * value
                for j in range(b):
                    old[4 * j] = old[4 * j] + now[0] * images[2 * j, k]
                    old[4 * j + 1] = old[4 * j + 1] + now[0] * images[2 * j + 1, k]
                    old[4 * j + 3] = old[4 * j + 3] + res_ref[k] * basis[2 * j, k]
            for k, prev, now, nxt in walk(solve(lambda k: y_ref[k], k_ref)):
                value = stencil(k, prev, now, nxt)
                w_ref[k] = value
                acc[4 + k % 2] = acc[4 + k % 2] + y_ref[k] * now[0]
                acc[6 + k % 2] = acc[6 + k % 2] + now[0] * value
                acc[8] = acc[8] + top_resp[k] * value
                for j in range(b):
                    old[4 * j + 2] = old[4 * j + 2] + now[0] * images[2 * j + 1, k]
            fields = [acc[2 * i] + acc[2 * i + 1] for i in range(4)] + old
            sums = jnp.zeros((1, width), jnp.float32)
            for i, x in enumerate(fields):
                sums = jnp.where(relative == own + i, total(jnp.where(own_row, x, 0.0)), sums)
            msg[b, 0] = both(last_row(z_ref[top]), last_row(k_ref[top]))
            msg[b, 1] = jnp.where(own_row, column_sum(acc[8]), sums)
            recv[b, me] = msg[b]
            send_rows(b)

            if b == 0:
                wait_for(stat_recv.at[0 : n_own - 1], stat_send, stat_arrive)
                h0, h1 = assemble(lambda spot: stat_recv[spot, 0])
                h2, north = assemble(lambda spot: stat_recv[spot, 1])
                ocean, _ = assemble(lambda spot: stat_recv[spot, 2])
                fold_open = 0.5 * (north + facing(north))
                fold_own = fold_open * ocean
                fold_far = fold_own * facing(ocean)
                h0_facing, own_facing = facing(h0), facing(fold_own)

            wait_for(recv.at[b, 0 : n_own - 1], send_sem.at[b], recv_sem.at[b])
            tau0, tau1 = assemble(lambda spot, b=b: recv[b, spot, 0])
            tail, rest_rows = assemble(lambda spot, b=b: recv[b, spot, 1])
            tau0_facing, tau1_facing = facing(tau0), facing(tau1)
            phi0 = fold_far * tau0_facing - fold_own * tau0
            phi0_facing = fold_far * tau0 - own_facing * tau0_facing
            top1 = tau1 - h0 * phi0
            phi1 = fold_far * (tau1_facing - h0_facing * phi0_facing) - fold_own * top1
            spread_phi = h1 * phi0 + h2 * east_whole(phi0) + west_whole(h2 * phi0)
            rest_sum = column_sum(rest_rows)

            def moment(i, x=None):
                row = jnp.where(rest_lane == i, rest_sum, 0.0)
                if x is not None:
                    row = row + column_sum(x)
                return jnp.sum(row, axis=1, keepdims=True)

            m0 = moment(0)
            m1 = moment(1, -tau0 * phi0)
            m2 = moment(2, phi0 * (h0 * phi0 - 2.0 * tau1))
            m3 = moment(3, phi0 * (spread_phi - 2.0 * tail) - top1 * phi1)
            cross, ends_of = [], []
            for j in range(b):
                first, mixed = moment(4 + 4 * j), moment(5 + 4 * j)
                last = moment(6 + 4 * j, -phi0 * tails[j])
                cross.append([[first, mixed], [mixed, last]])
                ends_of.append([moment(7 + 4 * j), first])
            ends_of.append([m0, m1])
            tails.append(tail - spread_phi - h0 * phi1)
            phi0_row, phi1_row = window(phi0), window(phi1)
            phi_rows.append(phi0_row)

            inner = [[m1, m2], [m2, m3]]
            pulls = []
            for j in range(b):
                against = cross[j]
                for i in range(j):
                    against = plus(against, turned_product(links[i, j], cross[i]))
                left = solve_pair(factors[j], against[0][0], against[1][0])
                right = solve_pair(factors[j], against[0][1], against[1][1])
                pulls.append([[left[0], right[0]], [left[1], right[1]]])
                inner = minus(inner, turned_product(against, pulls[j]))
            factors.append(factor(inner))
            for j in range(b):
                link = [[-x for x in row] for row in pulls[j]]
                for i in range(j + 1, b):
                    link = minus(link, product(links[j, i], pulls[i]))
                links[j, b] = link
            along = []
            for j in range(b + 1):
                u, v = ends_of[j]
                for i in range(j):
                    link, (p, q) = links[i, j], ends_of[i]
                    u = u + (link[0][0] * p + link[1][0] * q)
                    v = v + (link[0][1] * p + link[1][1] * q)
                along.append(solve_pair(factors[j], u, v))
            steps = []
            for j in range(b + 1):
                u, v = along[j]
                for i in range(j + 1, b + 1):
                    link, (p, q) = links[j, i], along[i]
                    u = u + (link[0][0] * p + link[0][1] * q)
                    v = v + (link[1][0] * p + link[1][1] * q)
                steps.append([u, v])
            for j in range(b + 1):
                weight_of[j] = [weight_of[j][i] + steps[j][i] for i in (0, 1)]
            wide_steps = [[spread(x) for x in row] for row in steps]
            p_mid, p_east, p_west = (
                spread(phi0_row),
                spread(east(phi0_row)),
                spread(west(phi0_row)),
            )
            phi1_top = jnp.where(is_top, spread(phi1_row), 0.0)
            phi0_top = jnp.where(is_top, p_mid, 0.0)
            final = b == blocks - 1
            if final:
                wide_weights = [[spread(x) for x in row] for row in weight_of]
                phi_sum = zero
                for j in range(blocks):
                    phi_sum = phi_sum + wide_weights[j][1] * phi_rows[j]
            for k in range(depth):
                image = y_ref[k]
                second = w_ref[k] - (c_mid[k] * p_mid + c_east[k] * p_east + c_west[k] * p_west)
                if k == top:
                    image = image - phi0_top
                    second = second - phi1_top
                value = res_ref[k] - (wide_steps[b][0] * image + wide_steps[b][1] * second)
                for j in range(b):
                    value = value - (
                        wide_steps[j][0] * images[2 * j, k]
                        + wide_steps[j][1] * images[2 * j + 1, k]
                    )
                if not final:
                    if k == top:
                        y_ref[k] = image
                    w_ref[k] = second
                    res_ref[k] = value
                    continue
                answer = -top_resp[k] * phi_sum
                for j in range(blocks):
                    answer = answer + (
                        wide_weights[j][0] * basis[2 * j, k]
                        + wide_weights[j][1] * basis[2 * j + 1, k]
                    )
                joined = jnp.where(own_row, answer, pltpu.roll(value, own, 1))
                back_msg[pl.ds(k, SUB, stride=depth), :] = joined

        for a in range(lat_count):

            @pl.when(jnp.logical_or(lat != a, lat < 2))
            def _(a=a):
                back_copy(a).start()

        @pl.when(lat >= 2)
        def _():
            back_recv[odd] = back_msg[pl.ds(pl.multiple_of(lat * rows, rows), rows), :]

        for a in range(lat_count):

            @pl.when(jnp.logical_or(lat != a, lat < 2))
            def _(a=a):
                back_copy(a).wait_send()

    pl.when(is_owner)(solve_columns)

    for c in range(FIELDS // 2):
        for side in range(2):
            pl.when(jnp.logical_not(big_stays[side]))(big_copy(side, c).wait_send)
        thin_copy(0, c).wait_send()
        pl.when(jnp.logical_not(thin_stays))(thin_copy(1, c).wait_send)

    for side in range(2):

        @pl.when(jnp.logical_or(core == 0, lat != 2 + side))
        def _(side=side):
            pltpu.make_async_remote_copy(
                src_ref=back_msg.at[0:rows],
                dst_ref=back_recv.at[side],
                send_sem=back_send.at[0],
                recv_sem=back_arrive.at[side],
                device_id=left_place,
                device_id_type=MESH,
            ).wait_recv()

    for v in range(rows // SUB):
        sl = slice(v * SUB, (v + 1) * SUB)
        first, second = back_recv[0, sl], back_recv[1, sl]
        sol_out[sl] = jnp.where(wide < own, first, second)
        res_out[sl] = pltpu.roll(jnp.where(wide < own, second, first), own, 1)


def shards(
    right_side,
    surface_term,
    east_coupling,
    north_coupling,
    neast_coupling,
    nwest_coupling,
    land_sea,
    fold_map,
):
    rows, width = right_side.shape
    lat_count = lax.axis_size("lat")
    lon_count = lax.axis_size("lon")
    n_own = lat_count * lon_count // 2
    depth = rows * lat_count // SUB
    subs = SUB // lat_count
    assert lat_count == 4 and ITERS % 2 == 0
    band = subs * (depth + SUB)
    thin = subs * SUB

    block = pltpu.VMEM((depth, SUB, width), jnp.float32)
    answer = pltpu.VMEM((rows, width), jnp.float32)
    vmem = pl.BlockSpec(memory_space=pltpu.VMEM)
    dma = pltpu.SemaphoreType.DMA

    def held(*shape):
        return pltpu.VMEM((*shape, width), jnp.float32)

    return pl.pallas_call(
        functools.partial(kernel, lat_count, lon_count),
        out_shape=(answer, answer),
        in_specs=[pl.BlockSpec(memory_space=pl.ANY)] * 8,
        out_specs=(vmem, vmem),
        scratch_shapes=[block] * 18
        + [
            held(ITERS, depth, SUB),
            held(ITERS, depth, SUB),
            *[held(depth, SUB)] * 7,
            held(FIELDS, rows),
            pltpu.VMEM((rows, width), jnp.int32),
            pltpu.SMEM((width,), jnp.int32),
            held(2, FIELDS // 2, band),
            held(2, FIELDS // 2, thin),
            held(FIELDS // 2, lat_count * band),
            held(FIELDS // 2, lat_count * thin),
            held(3, 1),
            held(n_own, 3, 1),
            held(ITERS // 2, 2, 1),
            held(ITERS // 2, n_own, 2, 1),
            held(lat_count * rows),
            held(2, rows),
            dma((FIELDS + 2,)),
            dma((2, FIELDS // 2)),
            dma((FIELDS // 2, lat_count)),
            dma((2, FIELDS // 2)),
            dma((FIELDS // 2, lat_count)),
            dma(()),
            dma(()),
            dma((ITERS // 2,)),
            dma((ITERS // 2,)),
            dma((lat_count,)),
            dma((2,)),
        ],
        compiler_params=pltpu.CompilerParams(collective_id=0, has_side_effects=True),
    )(
        right_side,
        surface_term,
        east_coupling,
        north_coupling,
        neast_coupling,
        nwest_coupling,
        land_sea,
        fold_map,
    )


def solution(mesh):
    return jax.shard_map(
        shards,
        mesh=mesh,
        in_specs=(P("lat", "lon"),) * 7 + (P("lon"),),
        out_specs=(P("lat", "lon"), P("lat", "lon")),
        check_vma=False,
    )
```

time: 45.7 us -> 39 us (0.85)
  Pallas kernels: 42.3 us -> 36.7 us
  local copies, waits for them, and re-layouts: 2.14 us -> 1.26 us
    pallas_call x1, Pallas kernels: 42.3 us -> 36.7 us  [shards(): pl.pallas_call(functools.partial(kernel, lat_count, lon_count), out_shape...]
    unnamed x4 -> x2, local copies, waits for them, and re-layouts: 2.14 us -> 1.26 us
where the time goes in v1:
time: 39 us; the launch traced here: 38.6 us
  Pallas kernels  36.7 us (94%)
  local copies, waits for them, and re-layouts  1.26 us (3%)
  between operations  0.64 us (2%)
    pallas_call x1, Pallas kernels, shards(): pl.pallas_call(functools.partial(kernel, lat_count, lon_count), out_shape...  36.7 us
    unnamed x2, local copies, waits for them, and re-layouts  1.26 us

profile of v1, /device:TPU:0, one launch (start us, length us, event | category | flops | bytes accessed | tf_op | source)
XLA Modules:
  0.0 38.6 jit_solution(7021873578197198233)
XLA Ops:
  0.6 36.7 %shard_map.95 = (f32[128,128]{1,0:T(8,128)S(1)}, f32[128,128]{1,0:T(8,128)S(1)}) custom-call(f32[128,128]{1,0:T(8,128)} %right_ref.1, f32[128,128]{1,0:T(8,128)} %surface_ref.1, f32[128,128]{1,0:T(8,128)} %east_ref.1, f32[128,128]{1,0:T(8,128)} %north_ref.1, f32[128,128]{1,0:T(8,128)} %neast_ref.1, f32[128,128]{1,0:T(8,128)} %nwest_ref.1, ...), custom_call_target="tpu_custom_call" | custom-call | tf_op jit(solution)/shard_map/pallas_call | solution.py:887
  37.3 0.6 %copy.12 = f32[128,128]{1,0:T(8,128)} copy(f32[128,128]{1,0:T(8,128)S(1)} %get-tuple-element.2) | data formatting | bytes 131072
  38.0 0.6 %copy.13 = f32[128,128]{1,0:T(8,128)} copy(f32[128,128]{1,0:T(8,128)S(1)} %get-tuple-element.3) | data formatting | bytes 131072
